TPU v7x, 128 devices: a whole 4x4x4 slice. The times are simulated.
128 devices in a mesh: group: 8 (over x, core), dev: 16 (over y, z).
Axes of the slice: x: 4, y: 4, z: 4, core: 2. Of those that a mesh axis runs over, the one named last changes fastest.
Arguments:
- images: bfloat16 [16384, 1152], P(('group', 'dev')), may hold values from -1 to 1
- texts: bfloat16 [16384, 1152], P(('group', 'dev')), may hold values from -1 to 1
- lang_order: int32 [16384], P(('group', 'dev')), may hold values from 0 to 2047, as said below
- position: int32 [16384], P(('group', 'dev')), may hold values from 0 to 2047, as said below
- logit_scale: float32 [1], replicated, may hold values from 8 to 24
- logit_bias: float32 [1], replicated, may hold values from -4 to -1
Outputs:
- image_grad: float32 [16384, 1152], P(('group', 'dev'))
- text_grad: float32 [16384, 1152], P(('group', 'dev'))
- loss: float32 [1], replicated
Inputs may be any that keep to these rules, and one draw needn't show every extreme that they name: In each group of 2048 examples, lang_order is a permutation of the group-local indices; the 128 entries of one device name at most 16 examples held by any one device of the group, and exactly 16 for each device they name. position is the inverse of lang_order within each group.
All inputs are finite; a program needn't handle non-finite values.
Results may differ from a plain program's by a relative error of at most 0.00062.
Values may be sent and summed in bfloat16 or wider, within the bound.
A program may use at most 64 MiB of HBM per device.

v0:
```python
import jax
import jax.numpy as jnp
from jax import lax
from jax.sharding import Mesh
from jax.sharding import PartitionSpec as P

DEV = ("dev_0", "dev_1")
GROUP = ("group_0", "group_1")
GROUP_DEV = ("group_0", "group_1", "dev_0", "dev_1")
EPSILON = 1e-06


def normalize(values):
    wide = values.astype(jnp.float32)
    recip = lax.rsqrt(jnp.sum(wide * wide, axis=1, keepdims=True) + EPSILON)
    return (wide * recip, recip)


def project_back(unit, recip, grad):
    return recip * (grad - unit * jnp.sum(unit * grad, axis=1, keepdims=True))


def per_device(images, texts, lang_order, position, logit_scale, logit_bias):
    row_count, width_count = images.shape
    dev_count = lax.axis_size(DEV)
    group_count = lax.axis_size(GROUP)
    scale = logit_scale[0]
    bias = logit_bias[0]
    span = row_count * dev_count
    group_index = lax.axis_index(GROUP)
    img_unit, img_recip = normalize(images)
    txt_unit, txt_recip = normalize(texts)
    img_block = lax.all_gather(img_unit.astype(jnp.bfloat16), DEV, axis=0, tiled=True)
    txt_block = lax.all_gather(txt_unit.astype(jnp.bfloat16), GROUP, axis=0, tiled=True)
    txt_ids = lax.all_gather(group_index * span + lang_order, GROUP, axis=0, tiled=True)
    img_ids = group_index * span + jnp.arange(span, dtype=jnp.int32)
    logits = (
        scale
        * lax.dot_general(
            img_block, txt_block, (((1,), (1,)), ((), ())), preferred_element_type=jnp.float32
        )
        + bias
    )
    sign = jnp.where(img_ids[:, None] == txt_ids[None, :], jnp.float32(1.0), jnp.float32(-1.0))
    loss_part = jnp.sum(-jax.nn.log_sigmoid(sign * logits))
    coeff = (-sign * jax.nn.sigmoid(-sign * logits)).astype(jnp.bfloat16)
    dimg_part = jnp.dot(coeff, txt_block, preferred_element_type=jnp.float32)
    dtext_part = lax.dot_general(
        coeff, img_block, (((0,), (0,)), ((), ())), preferred_element_type=jnp.float32
    )
    dimg = scale * lax.psum_scatter(dimg_part, DEV, scatter_dimension=0, tiled=True)
    dtext = scale * lax.psum_scatter(dtext_part, GROUP, scatter_dimension=0, tiled=True)
    total = jnp.float32(span * group_count)
    loss = (lax.psum(loss_part, GROUP_DEV) / (total * total)).reshape(1)
    return (project_back(img_unit, img_recip, dimg), project_back(txt_unit, txt_recip, dtext), loss)


def solution(mesh):
    finer = Mesh(mesh.devices.reshape(4, 2, 4, 4), GROUP_DEV)
    return jax.shard_map(
        per_device,
        mesh=finer,
        in_specs=(P(GROUP_DEV, None), P(GROUP_DEV, None), P(GROUP_DEV), P(GROUP_DEV), P(), P()),
        out_specs=(P(GROUP_DEV, None), P(GROUP_DEV, None), P()),
        check_vma=False,
    )
```

profile of v0, /device:TPU:0, one launch (start us, length us, event | category | flops | bytes accessed | tf_op | source)
XLA Modules:
  0.0 262.9 jit_solution(11099517485220100941)
XLA Ops:
  7.2 0.0 all-gather.6.cloned.1.call-start
  7.2 1.1 fusion.22
  8.3 1.8 fusion.11
  10.1 0.0 all-gather.6.cloned.1.call-update
  10.1 0.0 all-gather.4.cloned.1.call-start
  10.2 1.1 fusion.18
  11.3 1.8 fusion.14
  13.1 0.0 all-gather.4.cloned.1.call-update
  13.1 0.0 reduce-scatter.5.cloned.1.call-start
  14.5 0.7 add_bitcast_fusion
  15.1 10.6 %all-gather = s32[8,1,128]{2,1,0:T(1,128)S(1)} all-gather(s32[1,1,128]{2,1,0:T(1,128)S(1)} %add_bitcast_fusion), channel_id=1, replica_groups=mesh['group_0'=4,'group_1'=2,'dev_0'=4,'dev_1'=4] {'group_0','group_1'}, dimensions={0}, use_global_device_ids=true | all-gather | bytes 4608 | tf_op jit(solution)/shard_map/all_gather | solution.py:35
  25.8 12.5 %all-gather.6.cloned.1.call-done = bf16[1024,1152]{1,0:T(8,128)(2,1)} async-done(((bf16[128,1152]{1,0:T(8,128)(2,1)}), bf16[1024,1152]{1,0:T(8,128)(2,1)}) %all-gather.6.cloned.1.call-update) | async-done | bytes 2359312 | tf_op jit(solution)/shard_map/all_gather | solution.py:34
  38.3 57.3 %all-gather.4.cloned.1.call-done = bf16[2048,1152]{1,0:T(8,128)(2,1)} async-done(((bf16[128,1152]{1,0:T(8,128)(2,1)}), bf16[2048,1152]{1,0:T(8,128)(2,1)}) %all-gather.4.cloned.1.call-update) | async-done | bytes 4718608 | tf_op jit(solution)/shard_map/all_gather | solution.py:33
  95.6 0.0 copy-start.2
  95.6 16.4 %fusion.7 = (f32[]{:T(128)}, bf16[2048,1024]{1,0:T(8,128)(2,1)S(1)}) fusion(f32[]{:T(128)} %bitcast.17, f32[]{:T(128)} %bitcast.14, s32[1024]{0:T(1024)S(1)} %bitcast.18, s32[2048]{0:T(1024)S(1)} %iota_add_fusion, bf16[2048,1152]{1,0:T(8,128)(2,1)} %all-gather.4.cloned.1.call-done, bf16[1024,1152]{1,0:T(8,128)(2,1)} %all-gather.6.cloned.1.call-done), kind=kOutput, calls=%fused_computation.10 | convolution fusion | flops 4873781248 | bytes 11284492 | tf_op jit(solution)/shard_map/dot_general | solution.py:39
  112.0 1.9 copy-done.4
  113.9 0.0 copy-done.2
  113.9 7.6 %fusion.24 = f32[1024,1152]{1,0:T(8,128)} fusion(bf16[2048,1024]{1,0:T(8,128)(2,1)S(1)} %get-tuple-element.4, bf16[2048,1152]{1,0:T(8,128)(2,1)S(1)} %copy-done.2), kind=kOutput, calls=%fused_computation.36 | convolution fusion | flops 4831838208 | bytes 13631488 | tf_op jit(solution)/shard_map/dot_general | solution.py:48
  121.5 0.0 reduce-scatter.5.cloned.1.call-update
  121.5 0.0 reduce-scatter.3.cloned.1.call-start
  121.6 0.0 copy-done.3
  121.6 9.6 %fusion.23 = f32[2048,1152]{1,0:T(8,128)} fusion(bf16[2048,1024]{1,0:T(8,128)(2,1)} %copy-done.4, bf16[1024,1152]{1,0:T(8,128)(2,1)S(1)} %copy-done.3), kind=kOutput, calls=%fused_computation.35 | convolution fusion | flops 4831838208 | bytes 15990784 | tf_op jit(solution)/shard_map/dot_general | solution.py:47
  131.2 0.0 reduce-scatter.3.cloned.1.call-update
  131.2 65.9 %psum.7 = f32[]{:T(128)} all-reduce(f32[]{:T(128)} %get-tuple-element.3), channel_id=1, replica_groups=mesh['group_0'=4,'group_1'=2,'dev_0'=4,'dev_1'=4] {'group_0','group_1','..., use_global_device_ids=true, to_apply=%region_7.8 | all-reduce | flops 1 | bytes 8 | tf_op jit(solution)/shard_map/psum | solution.py:54
  197.7 0.0 reduce-scatter.5.cloned.1.call-done
  197.7 0.0 copy-done
  197.8 1.3 fusion.19
  199.1 2.1 fusion.21
  201.2 50.7 %reduce-scatter.3.cloned.1.call-done = f32[128,1152]{1,0:T(8,128)} async-done(((f32[2048,1152]{1,0:T(8,128)}), f32[128,1152]{1,0:T(8,128)}) %reduce-scatter.3.cloned.1.call-update) | async-done | bytes 589840 | tf_op jit(solution)/shard_map/reduce_scatter | solution.py:51
  251.8 0.0 copy-done.1
  251.8 1.3 fusion.15
  253.1 2.1 fusion.17
  (7 shorter events, 0.0 us)
Async XLA Ops:
  7.2 31.2 %all-gather.6.cloned.1.call-start = ((), (), s32[]{:S(2)}) async-start(), calls=%async_computation.3 | async-start | bytes 2654208 | tf_op jit(solution)/shard_map/all_gather | solution.py:34
  10.1 85.5 %all-gather.4.cloned.1.call-start = ((), (), s32[]{:S(2)}) async-start(), calls=%async_computation.2 | async-start | bytes 5013504 | tf_op jit(solution)/shard_map/all_gather | solution.py:33
  13.1 184.6 %reduce-scatter.5.cloned.1.call-start = ((), (), s32[]{:S(2)}) async-start(), calls=%async_computation.5 | async-start | bytes 5308416 | tf_op jit(solution)/shard_map/reduce_scatter | solution.py:52
  95.6 18.3 %copy-start.2 = (bf16[2048,1152]{1,0:T(8,128)(2,1)S(1)}, bf16[2048,1152]{1,0:T(8,128)(2,1)}, u32[]{:S(2)}) copy-start(bf16[2048,1152]{1,0:T(8,128)(2,1)} %all-gather.4.cloned.1.call-done) | copy-start | bytes 14155780
  112.0 1.9 copy-start.4
  113.9 7.6 %copy-start.3 = (bf16[1024,1152]{1,0:T(8,128)(2,1)S(1)}, bf16[1024,1152]{1,0:T(8,128)(2,1)}, u32[]{:S(2)}) copy-start(bf16[1024,1152]{1,0:T(8,128)(2,1)} %all-gather.6.cloned.1.call-done) | copy-start | bytes 7077892
  121.5 130.3 %reduce-scatter.3.cloned.1.call-start = ((), (), s32[]{:S(2)}) async-start(), calls=%async_computation.4 | async-start | bytes 10027008 | tf_op jit(solution)/shard_map/reduce_scatter | solution.py:51
  131.1 66.6 %copy-start = (bf16[128,1152]{1,0:T(8,128)(2,1)S(1)}, bf16[128,1152]{1,0:T(8,128)(2,1)}, u32[]{:S(2)}) copy-start(bf16[128,1152]{1,0:T(8,128)(2,1)} %param.7) | copy-start | bytes 884740
  131.1 120.7 %copy-start.1 = (bf16[128,1152]{1,0:T(8,128)(2,1)S(1)}, bf16[128,1152]{1,0:T(8,128)(2,1)}, u32[]{:S(2)}) copy-start(bf16[128,1152]{1,0:T(8,128)(2,1)} %param.6) | copy-start | bytes 884740
Sparse Core Ops, SparseCore 0:
  10.3 28.0 all-gather.5
  41.1 54.4 all-gather.3
  121.6 39.0 reduce-scatter.4
  164.1 87.6 reduce-scatter.2
where the time goes:
time: 263 us
  waiting for transfers between devices  121 us (46%)
  blocking collectives  76.5 us (29%)
  matrix products  33.5 us (13%)
  between operations  16.9 us (6%)
  other arithmetic  13.3 us (5%)
    psum x1, blocking collectives, per_device(): loss = (lax.psum(loss_part, GROUP_DEV) / (total * total)).reshape(1)  65.9 us
    all_gather x1, waiting for transfers between devices, per_device(): lax.all_gather(img_unit.astype(jnp.bfloat16), DEV, axis=0, tiled=True)  57.3 us
    reduce_scatter x1, waiting for transfers between devices, per_device(): lax.psum_scatter(dimg_part, DEV, scatter_dimension=0, tiled=True)  50.7 us
    dot_general x1, matrix products, per_device(): lax.dot_general(img_block, txt_block, (((1,), (1,)), ((), ())), preferred...  16.4 us
    all_gather x1, waiting for transfers between devices, per_device(): lax.all_gather(txt_unit.astype(jnp.bfloat16), GROUP, axis=0, tiled=True)  12.5 us
    all_gather x1, blocking collectives, per_device(): lax.all_gather(group_index * span + lang_order, GROUP, axis=0, tiled=True)  10.6 us
    dot_general x1, matrix products, per_device(): dimg_part = jnp.dot(coeff, txt_block, preferred_element_type=jnp.float32)  9.57 us
    dot_general x1, matrix products, per_device(): lax.dot_general(coeff, img_block, (((0,), (0,)), ((), ())), preferred_ele...  7.55 us
  transfers between devices with their start and end apart: 4, of which 3 were waited for; matrix products, arithmetic and copies ran while one was open for 6% of the time, Pallas kernels for 0%

commit v1 on v0

--- a/solution.py
+++ b/solution.py
@@ -30,7 +30,10 @@
     group_index = lax.axis_index(GROUP)
     img_unit, img_recip = normalize(images)
     txt_unit, txt_recip = normalize(texts)
-    img_block = lax.all_gather(img_unit.astype(jnp.bfloat16), DEV, axis=0, tiled=True)
+    img_block = jnp.concatenate(
+        lax.all_to_all(jnp.stack([img_unit.astype(jnp.bfloat16)] * lax.axis_size(DEV)), DEV, 0, 0),
+        axis=0,
+    )
     txt_block = lax.all_gather(txt_unit.astype(jnp.bfloat16), GROUP, axis=0, tiled=True)
     txt_ids = lax.all_gather(group_index * span + lang_order, GROUP, axis=0, tiled=True)
     img_ids = group_index * span + jnp.arange(span, dtype=jnp.int32)

time: 263 us -> 268 us (1.019)
  waiting for transfers between devices: 121 us -> 110 us
  starting transfers between devices: 0.16 us -> 8.51 us
  blocking collectives: 76.5 us -> 81.3 us
  other arithmetic: 13.3 us -> 10 us
  local copies, waits for them, and re-layouts: 1.96 us -> 4.76 us
    all_gather x1 -> x0, waiting for transfers between devices: 57.3 us -> none  [per_device(): lax.all_gather(img_unit.astype(jnp.bfloat16), DEV, axis=0, tiled=True)]
    all_to_all x0 -> x1, waiting for transfers between devices: none -> 41.7 us  [per_device(): lax.all_to_all(jnp.stack([img_unit.astype(jnp.bfloat16)] * lax.axis_size(...]
    all_to_all x0 -> x1, starting transfers between devices: none -> 8.2 us  [per_device(): lax.all_to_all(jnp.stack([img_unit.astype(jnp.bfloat16)] * lax.axis_size(...]
    psum x1, blocking collectives: 65.9 us -> 70.7 us  [per_device(): loss = (lax.psum(loss_part, GROUP_DEV) / (total * total)).reshape(1)]
    all_gather x1, waiting for transfers between devices: 12.5 us -> 17.1 us  [per_device(): lax.all_gather(txt_unit.astype(jnp.bfloat16), GROUP, axis=0, tiled=True)]
    another operation x0 -> x1, local copies, waits for them, and re-layouts: none -> 2.8 us  [per_device(): jnp.stack([img_unit.astype(jnp.bfloat16)] * lax.axis_size(DEV))]
  transfers between devices with their start and end apart: 4 -> 4, of which waited for: 3 -> 3; matrix products, arithmetic and copies ran while one was open for 6% -> 5% of each run, Pallas kernels for 0% -> 0%
where the time goes in v1:
time: 268 us
  waiting for transfers between devices  110 us (41%)
  blocking collectives  81.3 us (30%)
  matrix products  35.8 us (13%)
  between operations  16.9 us (6%)
  other arithmetic  10 us (4%)
  starting transfers between devices  8.51 us (3%)
  local copies, waits for them, and re-layouts  4.76 us (2%)
    psum x1, blocking collectives, per_device(): loss = (lax.psum(loss_part, GROUP_DEV) / (total * total)).reshape(1)  70.7 us
    reduce_scatter x1, waiting for transfers between devices, per_device(): lax.psum_scatter(dimg_part, DEV, scatter_dimension=0, tiled=True)  51.5 us
    all_to_all x1, waiting for transfers between devices, per_device(): lax.all_to_all(jnp.stack([img_unit.astype(jnp.bfloat16)] * lax.axis_size(...  41.7 us
    all_gather x1, waiting for transfers between devices, per_device(): lax.all_gather(txt_unit.astype(jnp.bfloat16), GROUP, axis=0, tiled=True)  17.1 us
    dot_general x1, matrix products, per_device(): lax.dot_general(img_block, txt_block, (((1,), (1,)), ((), ())), preferred...  16.2 us
    all_gather x1, blocking collectives, per_device(): lax.all_gather(group_index * span + lang_order, GROUP, axis=0, tiled=True)  10.6 us
    dot_general x1, matrix products, per_device(): lax.dot_general(coeff, img_block, (((0,), (0,)), ((), ())), preferred_ele...  10 us
    dot_general x1, matrix products, per_device(): dimg_part = jnp.dot(coeff, txt_block, preferred_element_type=jnp.float32)  9.57 us
  transfers between devices with their start and end apart: 4, of which 3 were waited for; matrix products, arithmetic and copies ran while one was open for 5% of the time, Pallas kernels for 0%

profile of v1, /device:TPU:0, one launch (start us, length us, event | category | flops | bytes accessed | tf_op | source)
XLA Modules:
  0.0 267.7 jit_solution(12037374779891629184)
XLA Ops:
  7.2 0.0 copy-start
  7.2 0.0 copy-start.3
  7.2 1.1 fusion.18
  8.3 1.1 fusion.14
  9.4 2.8 %stack.2 = bf16[16,128,1152]{2,1,0:T(8,128)(2,1)} broadcast(bf16[128,1152]{1,0:T(8,128)(2,1)S(1)} %fusion.14), dimensions={1,2} | broadcast | bytes 5013504 | tf_op jit(solution)/shard_map/stack | solution.py:34
  12.2 8.2 %all-to-all-start = ((bf16[16,128,1152]{2,1,0:T(8,128)(2,1)}), bf16[16,128,1152]{2,1,0:T(8,128)(2,1)}, u32[]{:S(2)}, u32[]{:S(2)}) async-start(bf16[16,128,1152]{2,1,0:T(8,128)(2,1)} %stack.2), calls=%async_computation | async-start | bytes 9437184 | tf_op jit(solution)/shard_map/all_to_all | solution.py:34
  20.4 0.0 all-gather.3.cloned.1.call-start
  20.5 0.0 copy-done
  20.5 0.1 fusion.22
  20.6 0.8 fusion.11
  21.5 0.0 all-gather.3.cloned.1.call-update
  21.5 0.0 reduce-scatter.5.cloned.1.call-start
  22.9 0.0 copy-done.3
  22.9 10.6 %all-gather = s32[8,1,128]{2,1,0:T(1,128)S(1)} all-gather(s32[1,1,128]{2,1,0:T(1,128)S(1)} %add_bitcast_fusion), channel_id=1, replica_groups=mesh['group_0'=4,'group_1'=2,'dev_0'=4,'dev_1'=4] {'group_0','group_1'}, dimensions={0}, use_global_device_ids=true | all-gather | bytes 4608 | tf_op jit(solution)/shard_map/all_gather | solution.py:38
  33.4 17.1 %all-gather.3.cloned.1.call-done = bf16[1024,1152]{1,0:T(8,128)(2,1)} async-done(((bf16[128,1152]{1,0:T(8,128)(2,1)}), bf16[1024,1152]{1,0:T(8,128)(2,1)}) %all-gather.3.cloned.1.call-update) | async-done | bytes 2359312 | tf_op jit(solution)/shard_map/all_gather | solution.py:37
  50.6 41.7 %all-to-all-done = bf16[16,128,1152]{2,1,0:T(8,128)(2,1)} async-done(((bf16[16,128,1152]{2,1,0:T(8,128)(2,1)}), bf16[16,128,1152]{2,1,0:T(8,128)(2,1)}, u32[]{:S(2)}, u32[]{:S(2)}) %all-to-all-start) | async-done | bytes 4718624 | tf_op jit(solution)/shard_map/all_to_all | solution.py:34
  92.3 16.2 %fusion.7 = (f32[]{:T(128)}, bf16[2048,1024]{1,0:T(8,128)(2,1)S(1)}) fusion(f32[]{:T(128)} %bitcast.18, f32[]{:T(128)} %bitcast.15, s32[1024]{0:T(1024)S(1)} %bitcast.19, s32[2048]{0:T(1024)S(1)} %iota_add_fusion, bf16[2048,1152]{1,0:T(8,128)(2,1)} %bitcast.3, bf16[1024,1152]{1,0:T(8,128)(2,1)} %all-gather.3.cloned.1.call-done), kind=kOutput, calls=%fused_computation.10 | convolution fusion | flops 4873781248 | bytes 11284492 | tf_op jit(solution)/shard_map/dot_general | solution.py:42
  108.5 1.9 copy-done.4
  110.5 10.0 %fusion.24 = f32[1024,1152]{1,0:T(8,128)} fusion(bf16[2048,1024]{1,0:T(8,128)(2,1)S(1)} %get-tuple-element.4, bf16[2048,1152]{1,0:T(8,128)(2,1)} %bitcast.3), kind=kOutput, calls=%fused_computation.36 | convolution fusion | flops 4831838208 | bytes 13631488 | tf_op jit(solution)/shard_map/dot_general | solution.py:51
  120.5 0.0 reduce-scatter.5.cloned.1.call-update
  120.5 0.2 reduce-scatter.3.cloned.1.call-start
  120.7 0.0 copy-done.2
  120.7 9.6 %fusion.23 = f32[2048,1152]{1,0:T(8,128)} fusion(bf16[2048,1024]{1,0:T(8,128)(2,1)} %copy-done.4, bf16[1024,1152]{1,0:T(8,128)(2,1)S(1)} %copy-done.2), kind=kOutput, calls=%fused_computation.35 | convolution fusion | flops 4831838208 | bytes 15990784 | tf_op jit(solution)/shard_map/dot_general | solution.py:50
  130.3 0.0 reduce-scatter.3.cloned.1.call-update
  130.3 70.7 %psum.7 = f32[]{:T(128)} all-reduce(f32[]{:T(128)} %get-tuple-element.3), channel_id=1, replica_groups=mesh['group_0'=4,'group_1'=2,'dev_0'=4,'dev_1'=4] {'group_0','group_1','..., use_global_device_ids=true, to_apply=%region_7.8 | all-reduce | flops 1 | bytes 8 | tf_op jit(solution)/shard_map/psum | solution.py:57
  201.7 0.0 reduce-scatter.5.cloned.1.call-done
  201.7 1.3 fusion.19
  203.0 2.1 fusion.21
  205.1 51.5 %reduce-scatter.3.cloned.1.call-done = f32[128,1152]{1,0:T(8,128)} async-done(((f32[2048,1152]{1,0:T(8,128)}), f32[128,1152]{1,0:T(8,128)}) %reduce-scatter.3.cloned.1.call-update) | async-done | bytes 589840 | tf_op jit(solution)/shard_map/reduce_scatter | solution.py:54
  256.6 0.0 copy-done.1
  256.6 1.3 fusion.15
  257.9 2.1 fusion.17
  (7 shorter events, 0.0 us)
Async XLA Ops:
  7.2 13.3 %copy-start = (bf16[128,1152]{1,0:T(8,128)(2,1)S(1)}, bf16[128,1152]{1,0:T(8,128)(2,1)}, u32[]{:S(2)}) copy-start(bf16[128,1152]{1,0:T(8,128)(2,1)} %param.7) | copy-start | bytes 884740
  7.2 15.7 %copy-start.3 = (s32[128]{0:T(128)S(1)}, s32[128]{0:T(128)}, u32[]{:S(2)}) copy-start(s32[128]{0:T(128)} %param.8) | copy-start | bytes 1540
  12.2 80.1 %all-to-all-start = ((bf16[16,128,1152]{2,1,0:T(8,128)(2,1)}), bf16[16,128,1152]{2,1,0:T(8,128)(2,1)}, u32[]{:S(2)}, u32[]{:S(2)}) async-start(bf16[16,128,1152]{2,1,0:T(8,128)(2,1)} %stack.2), calls=%async_computation | async-start | bytes 9437184 | tf_op jit(solution)/shard_map/all_to_all | solution.py:34
  20.4 30.2 %all-gather.3.cloned.1.call-start = ((), (), s32[]{:S(2)}) async-start(), calls=%async_computation.3 | async-start | bytes 2654208 | tf_op jit(solution)/shard_map/all_gather | solution.py:37
  21.5 180.2 %reduce-scatter.5.cloned.1.call-start = ((), (), s32[]{:S(2)}) async-start(), calls=%async_computation.5 | async-start | bytes 5308416 | tf_op jit(solution)/shard_map/reduce_scatter | solution.py:55
  108.5 1.9 copy-start.4
  110.5 10.3 %copy-start.2 = (bf16[1024,1152]{1,0:T(8,128)(2,1)S(1)}, bf16[1024,1152]{1,0:T(8,128)(2,1)}, u32[]{:S(2)}) copy-start(bf16[1024,1152]{1,0:T(8,128)(2,1)} %all-gather.3.cloned.1.call-done) | copy-start | bytes 7077892
  120.5 136.1 %reduce-scatter.3.cloned.1.call-start = ((), (), s32[]{:S(2)}) async-start(), calls=%async_computation.4 | async-start | bytes 10027008 | tf_op jit(solution)/shard_map/reduce_scatter | solution.py:54
  130.3 126.3 %copy-start.1 = (bf16[128,1152]{1,0:T(8,128)(2,1)S(1)}, bf16[128,1152]{1,0:T(8,128)(2,1)}, u32[]{:S(2)}) copy-start(bf16[128,1152]{1,0:T(8,128)(2,1)} %param.6) | copy-start | bytes 884740
Sparse Core Ops, SparseCore 0:
  23.5 27.0 all-gather.2
  120.6 44.6 reduce-scatter.4
  168.8 87.7 reduce-scatter.2
